TPU v7x, 256 devices: a whole 4x4x8 slice. The times are simulated.
256 devices in a mesh: replica: 64 (over z, x, core), model: 4 (over y).
Axes of the slice: x: 4, y: 4, z: 8, core: 2. Of those that a mesh axis runs over, the one named last changes fastest.
Arguments:
- partial_query: float32 [64, 1280, 1280], P('replica', None, 'model'), may hold values from -1.75 to 1.75
- partial_key: float32 [64, 1280, 1280], P('replica', None, 'model'), may hold values from -1.75 to 1.75
- partial_value: float32 [64, 1280, 1280], P('replica', None, 'model'), may hold values from -1.75 to 1.75
- partial_mixed: float32 [64, 1280, 1280], P('replica', 'model'), may hold values from -1.75 to 1.75
- partial_norm: float32 [64, 1280], P('replica'), may hold values from -16 to 16
- master_query: float32 [1280, 1280], P('replica', 'model'), may hold values from -0.15625 to 0.15625
- master_key: float32 [1280, 1280], P('replica', 'model'), may hold values from -0.15625 to 0.15625
- master_value: float32 [1280, 1280], P('replica', 'model'), may hold values from -0.15625 to 0.15625
- master_mixed: float32 [1280, 1280], P('model', 'replica'), may hold values from -0.15625 to 0.15625
- master_norm: float32 [1280], P('replica'), may hold values from 0.25 to 1.75
Outputs:
- compute_query: bfloat16 [1280, 1280], P(None, 'model')
- compute_key: bfloat16 [1280, 1280], P(None, 'model')
- compute_value: bfloat16 [1280, 1280], P(None, 'model')
- compute_mixed: bfloat16 [1280, 1280], P('model')
- compute_norm: bfloat16 [1280], replicated
- stepped_query: float32 [1280, 1280], P('replica', 'model')
- stepped_key: float32 [1280, 1280], P('replica', 'model')
- stepped_value: float32 [1280, 1280], P('replica', 'model')
- stepped_mixed: float32 [1280, 1280], P('model', 'replica')
- stepped_norm: float32 [1280], P('replica')
All inputs are finite; a program needn't handle non-finite values.
Results may differ from a plain program's by a relative error of at most 0.001.
Values may be sent and summed in bfloat16 or wider, within the bound.
No kernel may reach another device: no remote copies, remote signals or barrier semaphores. Data moves between devices by JAX's collectives and lax.ppermute only.
A program may use at most 128 MiB of HBM per device.

v0:
```python
import jax
import jax.numpy as jnp
from jax import lax
from jax.sharding import PartitionSpec as P

learn_rate = 0.3


def cut_along(x, dim, peers):
    before, after = (x.shape[:dim], x.shape[dim + 1 :])
    return jnp.moveaxis(x.reshape(*before, peers, -1, *after), dim, 0)


def sum_together(arrays, axis, dims):
    peers = lax.axis_size(axis)
    parts = [cut_along(a, dim, peers) for a, dim in zip(arrays, dims)]
    lines = jnp.concatenate([b.reshape(peers, -1) for b in parts], axis=1)
    extent = max(16, -(-lines.shape[1] // 1024) * 8)
    lines = jnp.pad(lines, ((0, 0), (0, extent * 128 - lines.shape[1]))).reshape(-1, 128)
    flat, at, finished = (lax.psum_scatter(lines, axis, tiled=True).reshape(-1), 0, [])
    for b in parts:
        part = b[0]
        finished.append(flat[at : at + part.size].reshape(part.shape))
        at += part.size
    return tuple(finished)


def gathered_total(x, axis):
    parts = lax.all_gather(x, axis)
    return parts.sum(axis=0)


def gather_turned(arrays, axis, dims):
    turned = [jnp.moveaxis(a, dim, 0) for a, dim in zip(arrays, dims)]
    both = jnp.concatenate([t.reshape(len(t), -1) for t in turned], axis=1)
    filled, at, finished = (lax.all_gather(both, axis, axis=0, tiled=True), 0, [])
    for t, dim in zip(turned, dims):
        share = filled[:, at : at + t[0].size].reshape(-1, *t.shape[1:])
        finished.append(jnp.moveaxis(share, 0, dim))
        at += t[0].size
    return tuple(finished)


def on_device(
    partial_query,
    partial_key,
    partial_value,
    partial_mixed,
    partial_norm,
    master_query,
    master_key,
    master_value,
    master_mixed,
    master_norm,
):
    mean_query, mean_key, mean_value, mean_mixed = sum_together(
        (partial_query[0], partial_key[0], partial_value[0], partial_mixed[0]),
        "replica",
        (0, 0, 0, 1),
    )
    whole_norm = gathered_total(partial_norm[0], "replica")
    place = lax.axis_index("replica")
    mean_norm = lax.dynamic_slice_in_dim(
        whole_norm, place * master_norm.shape[0], master_norm.shape[0]
    )
    mean_rate = lax.axis_size("replica") ** (-0.5)
    mean_query = mean_query * mean_rate
    mean_key = mean_key * mean_rate
    mean_value = mean_value * mean_rate
    mean_mixed = mean_mixed * mean_rate
    mean_norm = mean_norm * mean_rate
    stepped_query = master_query - learn_rate * mean_query
    stepped_key = master_key - learn_rate * mean_key
    stepped_value = master_value - learn_rate * mean_value
    stepped_mixed = master_mixed - learn_rate * mean_mixed
    stepped_norm = master_norm - learn_rate * mean_norm
    compute_query, compute_key, compute_value, compute_mixed, compute_norm = gather_turned(
        (
            stepped_query.astype(jnp.bfloat16),
            stepped_key.astype(jnp.bfloat16),
            stepped_value.astype(jnp.bfloat16),
            stepped_mixed.astype(jnp.bfloat16),
            stepped_norm.astype(jnp.bfloat16),
        ),
        "replica",
        (0, 0, 0, 1, 0),
    )
    return (
        compute_query,
        compute_key,
        compute_value,
        compute_mixed,
        compute_norm,
        stepped_query,
        stepped_key,
        stepped_value,
        stepped_mixed,
        stepped_norm,
    )


def solution(mesh):
    in_specs = (
        P("replica", None, "model"),
        P("replica", None, "model"),
        P("replica", None, "model"),
        P("replica", "model", None),
        P("replica", None),
        P("replica", "model"),
        P("replica", "model"),
        P("replica", "model"),
        P("model", "replica"),
        P("replica"),
    )
    out_specs = (
        P(None, "model"),
        P(None, "model"),
        P(None, "model"),
        P("model", None),
        P(),
        P("replica", "model"),
        P("replica", "model"),
        P("replica", "model"),
        P("model", "replica"),
        P("replica"),
    )
    return jax.shard_map(
        on_device, mesh=mesh, in_specs=in_specs, out_specs=out_specs, check_vma=False
    )
```

profile of v0, /device:TPU:1, one launch (start us, length us, event | category | flops | bytes accessed | tf_op | source)
XLA Modules:
  0.0 357.2 jit_solution(15330442983936035255)
XLA Ops:
  7.2 2.8 copy.59
  10.1 1.6 reshape_squeeze.3
  11.7 3.2 copy.60
  14.9 2.8 reshape.53
  17.8 2.1 copy.61
  19.9 1.8 copy.58
  21.7 2.2 reshape_reshape_squeeze.11
  24.0 1.8 copy.57
  25.8 2.1 reshape_reshape_squeeze.10
  27.9 1.8 copy.56
  29.8 2.2 reshape_reshape_squeeze.9
  32.0 4.8 %pad_maximum_fusion = f32[64,25600]{1,0:T(8,128)} fusion(f32[64,6400]{1,0:T(8,128)} %copy.61, f32[64,6400]{1,0:T(8,128)} %reshape_reshape_squeeze.11, f32[64,6400]{1,0:T(8,128)} %reshape_reshape_squeeze.10, f32[64,6400]{1,0:T(8,128)} %reshape_reshape_squeeze.9), kind=kLoop, calls=%fused_computation | loop fusion | flops 4915200 | bytes 13107200 | tf_op jit(solution)/shard_map/concatenate | solution.py:17
  36.8 6.4 %reshape.54 = f32[12800,128]{1,0:T(8,128)} reshape(f32[64,25600]{1,0:T(8,128)} %pad_maximum_fusion) | data formatting | bytes 13107200 | tf_op jit(solution)/shard_map/reshape | solution.py:19
  45.1 53.4 %all-gather = f32[64,1,1280]{2,1,0:T(1,128)S(1)} all-gather(f32[1,1,1280]{2,1,0:T(1,128)S(1)} %bitcast.16), channel_id=1, replica_groups=mesh['replica'=64,'model'=4] {'replica'}, dimensions={0}, use_global_device_ids=true | all-gather | bytes 332800 | tf_op jit(solution)/shard_map/all_gather | solution.py:29
  99.4 147.8 %all-reduce.3.cloned.1.call-done = f32[12800,128]{1,0:T(8,128)} async-done(((f32[12800,128]{1,0:T(8,128)}), f32[12800,128]{1,0:T(8,128)}) %all-reduce.3.cloned.1.call-update) | async-done | bytes 6553616
  247.1 0.9 dynamic-slice_multiply_fusion
  251.2 80.2 %all-gather.4.cloned.1.call-done = bf16[64,20,1281]{2,1,0:T(8,128)(2,1)} async-done(((bf16[1,20,1281]{2,1,0:T(8,128)(2,1)}), bf16[64,20,1281]{2,1,0:T(8,128)(2,1)}) %all-gather.4.cloned.1.call-update) | async-done | bytes 3279376 | tf_op jit(solution)/shard_map/all_gather | solution.py:36
  331.4 6.8 %reshape.60 = bf16[1280,1281]{1,0:T(8,128)(2,1)} reshape(bf16[64,20,1281]{2,1,0:T(8,128)(2,1)} %all-gather.4.cloned.1.call-done) | data formatting | bytes 6558720
  338.2 4.5 %slice_bitcast_fusion = (bf16[320,1280]{0,1:T(8,128)(2,1)S(1)}, bf16[1280,320]{1,0:T(8,128)(2,1)S(1)}, bf16[1280,320]{1,0:T(8,128)(2,1)S(1)}, bf16[1280,320]{1,0:T(8,128)(2,1)}) fusion(bf16[1280,1281]{1,0:T(8,128)(2,1)} %reshape.60), kind=kLoop, calls=%fused_computation.1 | loop fusion | bytes 6553600 | tf_op jit(solution)/shard_map/transpose | solution.py:39
  342.6 1.7 slice_reduce_fusion
  344.4 2.2 copy.64
  346.5 1.3 copy.65
  347.8 1.3 copy.66
  349.1 1.3 copy.67
  (31 shorter events, 5.3 us)
Async XLA Ops:
  7.2 240.0 %all-reduce.3.cloned.1.call-start = ((), (), s32[]{:S(2)}) async-start(), calls=%async_computation.1 | async-start | bytes 13107200
  43.2 0.7 copy-start.6
  43.2 1.9 copy-start.4
  43.2 55.5 %copy-start.5 = (f32[20]{0:T(128)S(1)}, f32[20]{0:T(128)}, u32[]{:S(2)}) copy-start(f32[20]{0:T(128)} %param.19) | copy-start | bytes 244
  43.2 205.4 %copy-start = (f32[20,320]{1,0:T(8,128)S(1)}, f32[20,320]{1,0:T(8,128)}, u32[]{:S(2)}) copy-start(f32[20,320]{1,0:T(8,128)} %param.15) | copy-start | bytes 76804
  43.2 206.0 %copy-start.1 = (f32[320,20]{0,1:T(8,128)S(1)}, f32[320,20]{0,1:T(8,128)}, u32[]{:S(2)}) copy-start(f32[320,20]{0,1:T(8,128)} %param.18) | copy-start | bytes 76804
  43.2 206.6 %copy-start.2 = (f32[20,320]{1,0:T(8,128)S(1)}, f32[20,320]{1,0:T(8,128)}, u32[]{:S(2)}) copy-start(f32[20,320]{1,0:T(8,128)} %param.17) | copy-start | bytes 76804
  43.2 206.6 %copy-start.3 = (f32[20,320]{1,0:T(8,128)S(1)}, f32[20,320]{1,0:T(8,128)}, u32[]{:S(2)}) copy-start(f32[20,320]{1,0:T(8,128)} %param.16) | copy-start | bytes 76804
  43.2 288.1 %all-gather.4.cloned.1.call-start = ((), (), s32[]{:S(2)}) async-start(), calls=%async_computation | async-start | bytes 4392960 | tf_op jit(solution)/shard_map/all_gather | solution.py:36
Sparse Core Ops, SparseCore 0:
  43.4 203.7 all-reduce.2
  251.3 79.9 all-gather.3
where the time goes:
time: 358 us; the launch traced here: 357 us
  waiting for transfers between devices  228 us (64%)
  blocking collectives  53.4 us (15%)
  local copies, waits for them, and re-layouts  52.5 us (15%)
  between operations  14.8 us (4%)
  other arithmetic  8.4 us (2%)
    unnamed x3, waiting for transfers between devices  148 us
    all_gather x1, waiting for transfers between devices, gather_turned(): lax.all_gather(both, axis, axis=0, tiled=True)  80.2 us
    all_gather x1, blocking collectives, gathered_total(): parts = lax.all_gather(x, axis)  53.4 us
    unnamed x24, local copies, waits for them, and re-layouts  22.2 us
  transfers between devices with their start and end apart: 2, of which 2 were waited for; matrix products, arithmetic and copies ran while one was open for 0% of the time, Pallas kernels for 0%

commit v1 on v0

--- a/solution.py
+++ b/solution.py
@@ -2,6 +2,7 @@
 import jax.numpy as jnp
 from jax import lax
 from jax.sharding import PartitionSpec as P
+from jax.lax import all_to_all, axis_size
 
 learn_rate = 0.3
 
@@ -33,7 +34,13 @@
 def gather_turned(arrays, axis, dims):
     turned = [jnp.moveaxis(a, dim, 0) for a, dim in zip(arrays, dims)]
     both = jnp.concatenate([t.reshape(len(t), -1) for t in turned], axis=1)
-    filled, at, finished = (lax.all_gather(both, axis, axis=0, tiled=True), 0, [])
+
+    def mark_terms(field_in):
+        w1 = jnp.stack([field_in for _ in range(axis_size(axis))], axis=0)
+        tile_out = all_to_all(w1, axis, 0, 0)
+        return jnp.concatenate(tile_out, axis=0)
+
+    filled, at, finished = (mark_terms(both), 0, [])
     for t, dim in zip(turned, dims):
         share = filled[:, at : at + t[0].size].reshape(-1, *t.shape[1:])
         finished.append(jnp.moveaxis(share, 0, dim))

time: 358 us -> 388 us (1.084)
  blocking collectives: 53.4 us -> 164 us
  waiting for transfers between devices: 228 us -> 148 us
    all_to_all x0 -> x1, blocking collectives: none -> 111 us  [mark_terms(): tile_out = all_to_all(w1, axis, 0, 0)]
    all_gather x1 -> x0, waiting for transfers between devices: 80.2 us -> none  [gather_turned(): lax.all_gather(both, axis, axis=0, tiled=True)]
    reshape x0 -> x1, local copies, waits for them, and re-layouts: none -> 6.79 us  [mark_terms(): return jnp.concatenate(tile_out, axis=0)]
    unnamed x24 -> x23, local copies, waits for them, and re-layouts: 22.2 us -> 15.5 us
    unnamed x3 -> x2, waiting for transfers between devices: 148 us -> 148 us
  transfers between devices with their start and end apart: 2 -> 1, of which waited for: 2 -> 1; matrix products, arithmetic and copies ran while one was open for 0% -> 0% of each run, Pallas kernels for 0% -> 0%
where the time goes in v1:
time: 388 us
  blocking collectives  164 us (42%)
  waiting for transfers between devices  148 us (38%)
  local copies, waits for them, and re-layouts  52.2 us (13%)
  between operations  14.8 us (4%)
  other arithmetic  8.4 us (2%)
    unnamed x2, waiting for transfers between devices  148 us
    all_to_all x1, blocking collectives, mark_terms(): tile_out = all_to_all(w1, axis, 0, 0)  111 us
    all_gather x1, blocking collectives, gathered_total(): parts = lax.all_gather(x, axis)  53.4 us
    unnamed x23, local copies, waits for them, and re-layouts  15.5 us
  transfers between devices with their start and end apart: 1, of which 1 were waited for; matrix products, arithmetic and copies ran while one was open for 0% of the time, Pallas kernels for 0%

profile of v1, /device:TPU:1, one launch (start us, length us, event | category | flops | bytes accessed | tf_op | source)
XLA Modules:
  0.0 387.6 jit_solution(17960639999276861835)
XLA Ops:
  7.2 2.8 copy.56
  10.1 1.6 reshape_squeeze.3
  11.7 3.3 copy.57
  14.9 2.8 reshape.58
  17.8 2.1 copy.58
  19.9 1.8 copy.55
  21.8 2.2 reshape_reshape_squeeze.11
  24.0 1.8 copy.54
  25.8 2.1 reshape_reshape_squeeze.10
  27.9 1.8 copy.53
  29.8 2.2 reshape_reshape_squeeze.9
  32.0 4.8 %pad_maximum_fusion = f32[64,25600]{1,0:T(8,128)} fusion(f32[64,6400]{1,0:T(8,128)} %copy.58, f32[64,6400]{1,0:T(8,128)} %reshape_reshape_squeeze.11, f32[64,6400]{1,0:T(8,128)} %reshape_reshape_squeeze.10, f32[64,6400]{1,0:T(8,128)} %reshape_reshape_squeeze.9), kind=kLoop, calls=%fused_computation | loop fusion | flops 4915200 | bytes 13107200 | tf_op jit(solution)/shard_map/concatenate | solution.py:18
  36.8 6.3 %reshape.59 = f32[12800,128]{1,0:T(8,128)} reshape(f32[64,25600]{1,0:T(8,128)} %pad_maximum_fusion) | data formatting | bytes 13107200 | tf_op jit(solution)/shard_map/reshape | solution.py:20
  45.0 53.4 %all-gather = f32[64,1,1280]{2,1,0:T(1,128)S(1)} all-gather(f32[1,1,1280]{2,1,0:T(1,128)S(1)} %bitcast.14), channel_id=1, replica_groups=mesh['replica'=64,'model'=4] {'replica'}, dimensions={0}, use_global_device_ids=true | all-gather | bytes 332800 | tf_op jit(solution)/shard_map/all_gather | solution.py:30
  99.3 147.8 %all-reduce.3.cloned.1.call-done = f32[12800,128]{1,0:T(8,128)} async-done(((f32[12800,128]{1,0:T(8,128)}), f32[12800,128]{1,0:T(8,128)}) %all-reduce.3.cloned.1.call-update) | async-done | bytes 6553616
  247.1 0.9 dynamic-slice_multiply_fusion
  250.8 111.0 %all_to_all.5 = bf16[64,20,1281]{2,1,0:T(8,128)(2,1)} all-to-all(bf16[64,20,1281]{2,1,0:T(8,128)(2,1)S(1)} %stack.2), channel_id=1, replica_groups=mesh['replica'=64,'model'=4] {'replica'}, dimensions={0} | all-to-all | bytes 6558720 | tf_op jit(solution)/shard_map/all_to_all | solution.py:40
  361.8 6.8 %reshape.61 = bf16[1280,1281]{1,0:T(8,128)(2,1)} reshape(bf16[64,20,1281]{2,1,0:T(8,128)(2,1)} %all_to_all.5) | data formatting | bytes 6558720 | tf_op jit(solution)/shard_map/reshape | solution.py:41
  368.6 4.5 %slice_bitcast_fusion = (bf16[320,1280]{0,1:T(8,128)(2,1)S(1)}, bf16[1280,320]{1,0:T(8,128)(2,1)S(1)}, bf16[1280,320]{1,0:T(8,128)(2,1)S(1)}, bf16[1280,320]{1,0:T(8,128)(2,1)}) fusion(bf16[1280,1281]{1,0:T(8,128)(2,1)} %reshape.61), kind=kLoop, calls=%fused_computation.1 | loop fusion | bytes 6553600 | tf_op jit(solution)/shard_map/transpose | solution.py:46
  373.0 1.7 slice_reduce_fusion
  374.8 2.2 copy.61
  376.9 1.3 copy.62
  378.2 1.3 copy.63
  379.5 1.3 copy.64
  (30 shorter events, 5.0 us)
Async XLA Ops:
  7.2 239.9 %all-reduce.3.cloned.1.call-start = ((), (), s32[]{:S(2)}) async-start(), calls=%async_computation.1 | async-start | bytes 13107200
  43.1 0.7 copy-start.6
  43.1 1.9 copy-start.4
  43.1 55.5 %copy-start.5 = (f32[20]{0:T(128)S(1)}, f32[20]{0:T(128)}, u32[]{:S(2)}) copy-start(f32[20]{0:T(128)} %param.19) | copy-start | bytes 244
  43.1 205.4 %copy-start = (f32[20,320]{1,0:T(8,128)S(1)}, f32[20,320]{1,0:T(8,128)}, u32[]{:S(2)}) copy-start(f32[20,320]{1,0:T(8,128)} %param.15) | copy-start | bytes 76804
  43.1 206.0 %copy-start.1 = (f32[320,20]{0,1:T(8,128)S(1)}, f32[320,20]{0,1:T(8,128)}, u32[]{:S(2)}) copy-start(f32[320,20]{0,1:T(8,128)} %param.18) | copy-start | bytes 76804
  43.1 206.6 %copy-start.2 = (f32[20,320]{1,0:T(8,128)S(1)}, f32[20,320]{1,0:T(8,128)}, u32[]{:S(2)}) copy-start(f32[20,320]{1,0:T(8,128)} %param.17) | copy-start | bytes 76804
  43.2 206.6 %copy-start.3 = (f32[20,320]{1,0:T(8,128)S(1)}, f32[20,320]{1,0:T(8,128)}, u32[]{:S(2)}) copy-start(f32[20,320]{1,0:T(8,128)} %param.16) | copy-start | bytes 76804
Sparse Core Ops, SparseCore 0:
  43.3 203.7 all-reduce.2
